TPU v7x, 512 devices: a 8x2x16 block of a 8x8x16 slice. The times are simulated.
512 devices in a mesh: grp: 2 (over y), seq: 128 (over z, x), head: 2 (over core).
Axes of the slice: x: 8, y: 2, z: 16, core: 2. Of those that a mesh axis runs over, the one named last changes fastest.
The devices are a block of a 8x8x16 slice.
Arguments:
- key_cache: bfloat16 [4, 1024, 128, 1024], P('grp', ('seq', 'head')), parts along dimension 0, may hold values from -160 to 160, as said below
- value_cache: bfloat16 [4, 1024, 128, 1024], P('grp', ('seq', 'head')), parts along dimension 0, may hold values from -16 to 16, as said below
- query: bfloat16 [4, 4096], P('grp', 'head'), parts along dimension 0, may hold values from -48 to 48, as said below
- lengths: int32 [4], P('grp'), parts along dimension 0, may hold values from 128 to 131072, as said below
- block_map: int32 [4, 1024], P('grp'), parts along dimension 0, may hold values from 0 to 1023, each once within a row
Outputs:
- attended: bfloat16 [4, 4096], P('grp', 'head'), parts along dimension 0
There are 2 independent parts, one for each index of `grp`. A program takes and returns all parts, laid end to end along the dimension named above; each array names one. Nothing has to cross between parts.
Inputs may be any that keep to these rules, and one draw needn't show every extreme that they name: `lengths`: every length is a multiple of 128; in every draw some request has length 131072. `key_cache`: finite entries, drawn afresh for every request, block, token and channel. `value_cache`: finite entries, drawn afresh for every request, block, token and channel. `query`: finite entries, drawn afresh for every request, head and channel.
All inputs are finite; a program needn't handle non-finite values.
Results may differ from a plain program's by a relative error of at most 0.0055.
Values may be sent and summed in bfloat16 or wider, within the bound.
No kernel may reach another device: no remote copies, remote signals or barrier semaphores. Data moves between devices by JAX's collectives and lax.ppermute only.
A program may use at most 64 MiB of HBM per device.

v0:
```python
import jax
import jax.numpy as jnp
from jax import lax
from jax.sharding import Mesh
from jax.sharding import PartitionSpec as P

QH = 32
KVH = 8
HD = 128
BLK = 128
SEQ = ("seq_0", "seq_1")
SEQ_HEAD = ("seq_0", "seq_1", "head")


def all_in_one(shard, axis):
    leaves = jax.tree.leaves(shard)
    sequence = sorted(range(len(leaves)), key=lambda k: -leaves[k].size)
    width = (1, *leaves[sequence[0]].shape)[-1]
    lines = [
        jnp.pad(leaves[k].reshape(-1), (0, -leaves[k].size % width)).reshape(-1, width)
        for k in sequence
    ]
    both, at, found = (lax.all_gather(jnp.concatenate(lines), axis), 0, {})
    for k, line in zip(sequence, lines):
        share = both[:, at : at + len(line)].reshape(len(both), -1)
        found[k] = share[:, : leaves[k].size].reshape(-1, *leaves[k].shape)
        at += len(line)
    numbers = iter(range(len(leaves)))
    return jax.tree.map(lambda _: found[next(numbers)], shard)


def combined_by_axis(shard, axes, combine):
    for axis in axes:
        pieces = all_in_one(shard, axis)
        shard = jax.tree.map(lambda part: part[0], pieces)
        for k in range(1, lax.axis_size(axis)):
            shard = combine(shard, jax.tree.map(lambda part: part[k], pieces))
    return shard


def combine(earlier, later):
    top_new = jnp.maximum(earlier[0], later[0])
    factor_a = jnp.exp(earlier[0] - top_new)
    factor_b = jnp.exp(later[0] - top_new)
    total = earlier[1] * factor_a + later[1] * factor_b
    summed_values = earlier[2] * factor_a[..., None] + later[2] * factor_b[..., None]
    return (top_new, total, summed_values)


def partials(key_rows, value_rows, queries, live_blocks):
    batch_rows = key_rows.shape[0]
    slot_count = key_rows.shape[1]
    group_count = key_rows.shape[3] // HD
    token_count = slot_count * BLK
    key_flat = key_rows.reshape(batch_rows, token_count, group_count, HD)
    value_flat = value_rows.reshape(batch_rows, token_count, group_count, HD)
    query_heads = queries.reshape(batch_rows, group_count, QH // KVH, HD)
    logit_scores = jnp.einsum(
        "bgqd,btgd->bgqt", query_heads, key_flat, preferred_element_type=jnp.float32
    )
    logit_scores = logit_scores * (1.0 / HD**0.5)
    logit_scores = logit_scores.reshape(batch_rows, group_count, QH // KVH, slot_count, BLK)
    live_mask = live_blocks[:, None, None, :, None]
    row_top = jnp.max(jnp.where(live_mask, logit_scores, jnp.float32(-1e30)), axis=(3, 4))
    expo = jnp.where(live_mask, jnp.exp(logit_scores - row_top[..., None, None]), jnp.float32(0.0))
    total = jnp.sum(expo, axis=(3, 4))
    weights = expo.astype(jnp.bfloat16).reshape(batch_rows, group_count, QH // KVH, token_count)
    summed_values = jnp.einsum(
        "bgqt,btgd->bgqd", weights, value_flat, preferred_element_type=jnp.float32
    )
    return (row_top, total, summed_values)


def owned_live(block_map, lengths, position, count):
    owned_blocks = lax.dynamic_slice_in_dim(block_map, position * count, count, 1)
    return owned_blocks < (lengths // BLK)[:, None]


def on_device(key_cache, value_cache, query, lengths, block_map):
    batch_rows = key_cache.shape[0]
    width_here = query.shape[1]
    key_rows, value_rows = (
        lax.all_to_all(key_cache, "head", split_axis=3, concat_axis=1, tiled=True),
        lax.all_to_all(value_cache, "head", split_axis=3, concat_axis=1, tiled=True),
    )
    live_blocks = owned_live(block_map, lengths, lax.axis_index(SEQ), key_rows.shape[1])
    local = partials(key_rows, value_rows, query, live_blocks)
    row_top, total, summed_values = combined_by_axis(local, SEQ, combine)
    result = summed_values / total[..., None]
    return result.reshape(batch_rows, width_here).astype(jnp.bfloat16)


def solution(mesh):
    torus = Mesh(
        mesh.devices.reshape(mesh.shape["grp"], 16, 8, mesh.shape["head"]),
        ("grp", "seq_0", "seq_1", "head"),
    )
    placed = (
        P("grp", SEQ_HEAD, None, None),
        P("grp", SEQ_HEAD, None, None),
        P("grp", "head"),
        P("grp"),
        P("grp", None),
    )
    return jax.shard_map(
        on_device, mesh=torus, in_specs=placed, out_specs=P("grp", "head"), check_vma=False
    )
```

profile of v0, /device:TPU:80, one launch (start us, length us, event | category | flops | bytes accessed | tf_op | source)
XLA Modules:
  0.0 132.9 jit_solution(2421228417511749975)
XLA Ops:
  0.0 4.3 %copy.10 = bf16[2,4,128,1024]{2,1,0,3:T(4,128)(2,1)} copy(bf16[2,4,128,1024]{3,2,1,0:T(8,128)(2,1)} %param.5) | data formatting | bytes 4194304 | tf_op args[0]
  4.3 3.9 %all-to-all-start = ((bf16[2,4,128,1024]{2,1,0,3:T(4,128)(2,1)}), bf16[2,4,128,1024]{2,1,0,3:T(4,128)(2,1)S(1)}, u32[]{:S(2)}, u32[]{:S(2)}) async-start(bf16[2,4,128,1024]{2,1,0,3:T(4,128)(2,1)} %copy.10), calls=%async_computation | async-start | bytes 4194304 | tf_op jit(solution)/shard_map/all_to_all | solution.py:83
  8.3 0.8 dynamic-slice_compare_fusion
  9.2 4.3 %copy.13 = bf16[2,4,128,1024]{2,1,0,3:T(4,128)(2,1)} copy(bf16[2,4,128,1024]{3,2,1,0:T(8,128)(2,1)} %param.6) | data formatting | bytes 4194304 | tf_op args[1]
  13.5 4.8 %all-to-all-start.1 = ((bf16[2,4,128,1024]{2,1,0,3:T(4,128)(2,1)}), bf16[2,4,128,1024]{2,1,0,3:T(4,128)(2,1)}, u32[]{:S(2)}, u32[]{:S(2)}) async-start(bf16[2,4,128,1024]{2,1,0,3:T(4,128)(2,1)} %copy.13), calls=%async_computation.1 | async-start | bytes 4194304 | tf_op jit(solution)/shard_map/all_to_all | solution.py:84
  18.3 3.0 %copy.11 = bf16[2,4,128,2,512]{4,2,1,3,0:T(8,128)(2,1)} copy(bf16[2,4,128,2,512]{2,1,0,4,3:T(4,128)(2,1)S(1)} %bitcast.574) | data formatting | bytes 4194304 | tf_op jit(solution)/shard_map/all_to_all | solution.py:83
  21.4 2.5 %reshape.1675 = bf16[2,1024,4,128]{3,2,1,0:T(4,128)(2,1)S(1)} reshape(bf16[2,2,4,128,512]{4,3,2,1,0:T(8,128)(2,1)} %bitcast.575) | data formatting | bytes 4194304 | tf_op jit(solution)/shard_map/reshape | solution.py:55
  23.9 0.7 select_reduce_fusion
  24.7 0.2 fusion.7
  25.0 3.0 %copy.14 = bf16[2,4,128,2,512]{4,2,1,3,0:T(8,128)(2,1)S(1)} copy(bf16[2,4,128,2,512]{2,1,0,4,3:T(4,128)(2,1)} %bitcast.2) | data formatting | bytes 4194304 | tf_op jit(solution)/shard_map/all_to_all | solution.py:84
  28.0 2.1 %reshape.1676 = bf16[2,1024,4,128]{3,2,1,0:T(4,128)(2,1)} reshape(bf16[2,2,4,128,512]{4,3,2,1,0:T(8,128)(2,1)S(1)} %bitcast.576) | data formatting | bytes 4194304 | tf_op jit(solution)/shard_map/reshape | solution.py:56
  30.1 2.1 %fusion = f32[2,4,4,128]{3,2,1,0:T(4,128)S(1)} fusion(bf16[2,1024,4,128]{3,2,1,0:T(4,128)(2,1)} %reshape.1676, f32[2,4,4,1024]{3,2,1,0:T(4,128)S(1)} %get-tuple-element.91, f32[2,4,4]{2,1,0:T(4,128)S(1)} %get-tuple-element.90, pred[2,1024]{1,0:T(4,128)(4,1)S(1)} %bitcast.619), kind=kOutput, calls=%fused_computation | convolution fusion | flops 8486912 | bytes 2246784 | tf_op jit(solution)/shard_map/bgqt,btgd->bgqd/dot_general | solution.py:68
  32.2 69.8 %all-gather.2 = f32[16,34,128]{2,1,0:T(8,128)S(1)} all-gather(f32[1,34,128]{2,1,0:T(8,128)S(1)} %maximum_bitcast_fusion), channel_id=2, replica_groups=mesh['grp'=2,'seq_0'=16,'seq_1'=8,'head'=2] {'seq_0'}, dimensions={0}, use_global_device_ids=true | all-gather | bytes 295936 | tf_op jit(solution)/shard_map/all_gather | solution.py:23
  102.2 0.2 fusion.14
  102.4 26.6 %all-gather.3 = f32[8,34,128]{2,1,0:T(8,128)S(1)} all-gather(f32[1,34,128]{2,1,0:T(8,128)S(1)} %maximum_bitcast_fusion.1), channel_id=3, replica_groups=mesh['grp'=2,'seq_0'=16,'seq_1'=8,'head'=2] {'seq_1'}, dimensions={0}, use_global_device_ids=true | all-gather | bytes 156672 | tf_op jit(solution)/shard_map/all_gather | solution.py:23
  129.5 0.1 squeeze.268
  129.6 0.1 squeeze.266
  129.7 0.1 squeeze.265
  129.8 0.1 squeeze.278
  129.9 0.1 squeeze.287
  130.0 0.1 squeeze.286
  130.1 0.1 squeeze.285
  130.2 0.1 squeeze.283
  132.2 0.7 fusion.58
  (72 shorter events, 2.8 us)
Async XLA Ops:
  4.3 3.9 %copy-start.1 = (s32[2]{0:T(128)S(1)}, s32[2]{0:T(128)}, u32[]{:S(2)}) copy-start(s32[2]{0:T(128)} %param.8) | copy-start | bytes 28
  4.3 4.8 %copy-start = (bf16[2,2048]{1,0:T(2,128)(2,1)S(1)}, bf16[2,2048]{1,0:T(2,128)(2,1)}, u32[]{:S(2)}) copy-start(bf16[2,2048]{1,0:T(2,128)(2,1)} %param.7) | copy-start | bytes 24580
  4.3 9.1 %all-to-all-start = ((bf16[2,4,128,1024]{2,1,0,3:T(4,128)(2,1)}), bf16[2,4,128,1024]{2,1,0,3:T(4,128)(2,1)S(1)}, u32[]{:S(2)}, u32[]{:S(2)}) async-start(bf16[2,4,128,1024]{2,1,0,3:T(4,128)(2,1)} %copy.10), calls=%async_computation | async-start | bytes 4194304 | tf_op jit(solution)/shard_map/all_to_all | solution.py:83
  13.5 11.6 %all-to-all-start.1 = ((bf16[2,4,128,1024]{2,1,0,3:T(4,128)(2,1)}), bf16[2,4,128,1024]{2,1,0,3:T(4,128)(2,1)}, u32[]{:S(2)}, u32[]{:S(2)}) async-start(bf16[2,4,128,1024]{2,1,0,3:T(4,128)(2,1)} %copy.13), calls=%async_computation.1 | async-start | bytes 4194304 | tf_op jit(solution)/shard_map/all_to_all | solution.py:84
where the time goes:
time: 133 us
  blocking collectives  96.4 us (72%)
  local copies, waits for them, and re-layouts  22.6 us (17%)
  starting transfers between devices  8.77 us (7%)
  matrix products  2.8 us (2%)
  other arithmetic  2.06 us (2%)
    all_gather x2, blocking collectives, all_in_one(): both, at, found = (lax.all_gather(jnp.concatenate(lines), axis), 0, {})  96.4 us
    unnamed x8, local copies, waits for them, and re-layouts  8.7 us
    all_to_all x1, starting transfers between devices, on_device(): lax.all_to_all(value_cache, 'head', split_axis=3, concat_axis=1, tiled=True)  4.84 us
    all_to_all x1, starting transfers between devices, on_device(): lax.all_to_all(key_cache, 'head', split_axis=3, concat_axis=1, tiled=True)  3.92 us
    all_to_all x1, local copies, waits for them, and re-layouts, on_device(): lax.all_to_all(key_cache, 'head', split_axis=3, concat_axis=1, tiled=True)  3.04 us
    all_to_all x1, local copies, waits for them, and re-layouts, on_device(): lax.all_to_all(value_cache, 'head', split_axis=3, concat_axis=1, tiled=True)  2.98 us
  transfers between devices with their start and end apart: 2, of which 0 were waited for; matrix products, arithmetic and copies ran while one was open for 9% of the time, Pallas kernels for 0%

commit v1 on v0

--- a/solution.py
+++ b/solution.py
@@ -81,7 +81,12 @@
     width_here = query.shape[1]
     key_rows, value_rows = (
         lax.all_to_all(key_cache, "head", split_axis=3, concat_axis=1, tiled=True),
-        lax.all_to_all(value_cache, "head", split_axis=3, concat_axis=1, tiled=True),
+        jnp.concatenate(
+            lax.all_to_all(
+                jnp.stack(jnp.split(value_cache, lax.axis_size("head"), axis=3)), "head", 0, 0
+            ),
+            axis=1,
+        ),
     )
     live_blocks = owned_live(block_map, lengths, lax.axis_index(SEQ), key_rows.shape[1])
     local = partials(key_rows, value_rows, query, live_blocks)

time: 133 us -> 131 us (0.985)
  local copies, waits for them, and re-layouts: 22.6 us -> 18.8 us
  other arithmetic: 2.06 us -> 3.6 us
    unnamed x8 -> x7, local copies, waits for them, and re-layouts: 8.7 us -> 4.4 us
    another operation x0 -> x2, local copies, waits for them, and re-layouts: none -> 3.83 us  [the longest x1 2.09 us: partials(): value_flat = value_rows.reshape(batch_rows, token_count, group_count, HD)]
    all_to_all x1 -> x0, local copies, waits for them, and re-layouts: 2.98 us -> none  [on_device(): lax.all_to_all(value_cache, 'head', split_axis=3, concat_axis=1, tiled=True)]
    another operation x0 -> x1, other arithmetic: none -> 1.54 us  [on_device(): jnp.stack(jnp.split(value_cache, lax.axis_size('head'), axis=3))]
  transfers between devices with their start and end apart: 2 -> 2, of which waited for: 0 -> 0; matrix products, arithmetic and copies ran while one was open for 9% -> 8% of each run, Pallas kernels for 0% -> 0%
where the time goes in v1:
time: 131 us
  blocking collectives  96.4 us (74%)
  local copies, waits for them, and re-layouts  18.8 us (14%)
  starting transfers between devices  8.77 us (7%)
  other arithmetic  3.6 us (3%)
  matrix products  2.8 us (2%)
    all_gather x2, blocking collectives, all_in_one(): both, at, found = (lax.all_gather(jnp.concatenate(lines), axis), 0, {})  96.4 us
    all_to_all x1, starting transfers between devices, on_device(): lax.all_to_all(jnp.stack(jnp.split(value_cache, lax.axis_size('head'), ax...  4.84 us
    unnamed x7, local copies, waits for them, and re-layouts  4.4 us
    all_to_all x1, starting transfers between devices, on_device(): lax.all_to_all(key_cache, 'head', split_axis=3, concat_axis=1, tiled=True)  3.92 us
    all_to_all x1, local copies, waits for them, and re-layouts, on_device(): lax.all_to_all(key_cache, 'head', split_axis=3, concat_axis=1, tiled=True)  3.04 us
  transfers between devices with their start and end apart: 2, of which 0 were waited for; matrix products, arithmetic and copies ran while one was open for 8% of the time, Pallas kernels for 0%

profile of v1, /device:TPU:80, one launch (start us, length us, event | category | flops | bytes accessed | tf_op | source)
XLA Modules:
  0.0 130.7 jit_solution(3574117170436312253)
XLA Ops:
  0.0 4.3 %copy.10 = bf16[2,4,128,1024]{2,1,0,3:T(4,128)(2,1)} copy(bf16[2,4,128,1024]{3,2,1,0:T(8,128)(2,1)} %param.5) | data formatting | bytes 4194304 | tf_op args[0]
  4.3 3.9 %all-to-all-start = ((bf16[2,4,128,1024]{2,1,0,3:T(4,128)(2,1)}), bf16[2,4,128,1024]{2,1,0,3:T(4,128)(2,1)S(1)}, u32[]{:S(2)}, u32[]{:S(2)}) async-start(bf16[2,4,128,1024]{2,1,0,3:T(4,128)(2,1)} %copy.10), calls=%async_computation | async-start | bytes 4194304 | tf_op jit(solution)/shard_map/all_to_all | solution.py:83
  8.3 0.8 dynamic-slice_compare_fusion
  9.2 1.7 %slice_bitcast_fusion.1 = (bf16[1,2,4,128,512]{4,3,2,1,0:T(8,128)(2,1)S(1)}, bf16[1,2,4,128,512]{4,3,2,1,0:T(8,128)(2,1)S(1)}) fusion(bf16[2,4,128,1024]{3,2,1,0:T(8,128)(2,1)} %param.6), kind=kLoop, calls=%fused_computation.7 | loop fusion | bytes 4194304 | tf_op jit(solution)/shard_map/stack | solution.py:86
  10.9 1.5 %pad_maximum_fusion = bf16[2,2,4,128,512]{4,3,2,1,0:T(8,128)(2,1)} fusion(bf16[1,2,4,128,512]{4,3,2,1,0:T(8,128)(2,1)S(1)} %get-tuple-element.79, bf16[1,2,4,128,512]{4,3,2,1,0:T(8,128)(2,1)S(1)} %get-tuple-element.78), kind=kLoop, calls=%fused_computation | loop fusion | flops 1048576 | bytes 4194304 | tf_op jit(solution)/shard_map/stack | solution.py:86
  12.4 4.8 %all-to-all-start.1 = ((bf16[2,2,4,128,512]{4,3,2,1,0:T(8,128)(2,1)}), bf16[2,2,4,128,512]{4,3,2,1,0:T(8,128)(2,1)}, u32[]{:S(2)}, u32[]{:S(2)}) async-start(bf16[2,2,4,128,512]{4,3,2,1,0:T(8,128)(2,1)} %pad_maximum_fusion), calls=%async_computation.1 | async-start | bytes 4194304 | tf_op jit(solution)/shard_map/all_to_all | solution.py:85
  17.3 3.0 %copy.11 = bf16[2,4,128,2,512]{4,2,1,3,0:T(8,128)(2,1)} copy(bf16[2,4,128,2,512]{2,1,0,4,3:T(4,128)(2,1)S(1)} %bitcast.577) | data formatting | bytes 4194304 | tf_op jit(solution)/shard_map/all_to_all | solution.py:83
  20.3 2.5 %reshape.1674 = bf16[2,1024,4,128]{3,2,1,0:T(4,128)(2,1)S(1)} reshape(bf16[2,2,4,128,512]{4,3,2,1,0:T(8,128)(2,1)} %bitcast.578) | data formatting | bytes 4194304 | tf_op jit(solution)/shard_map/reshape | solution.py:55
  22.9 0.7 select_reduce_fusion
  23.7 0.2 fusion.7
  24.0 1.8 %copy.13 = bf16[2,2,4,128,512]{4,3,2,1,0:T(8,128)(2,1)S(1)} copy(bf16[2,2,4,128,512]{4,3,2,0,1:T(8,128)(2,1)} %bitcast.4) | data formatting | bytes 4194304 | tf_op jit(solution)/shard_map/reshape | solution.py:84
  25.8 2.1 %reshape_reshape.2 = bf16[2,1024,4,128]{3,2,1,0:T(4,128)(2,1)} reshape(bf16[2,2,4,128,512]{4,3,2,1,0:T(8,128)(2,1)S(1)} %copy.13) | data formatting | bytes 4194304 | tf_op jit(solution)/shard_map/reshape;reshape | solution.py:56
  27.9 2.1 %fusion = f32[2,4,4,128]{3,2,1,0:T(4,128)S(1)} fusion(bf16[2,1024,4,128]{3,2,1,0:T(4,128)(2,1)} %reshape_reshape.2, f32[2,4,4,1024]{3,2,1,0:T(4,128)S(1)} %get-tuple-element.93, f32[2,4,4]{2,1,0:T(4,128)S(1)} %get-tuple-element.92, pred[2,1024]{1,0:T(4,128)(4,1)S(1)} %bitcast.616), kind=kOutput, calls=%fused_computation.1 | convolution fusion | flops 8486912 | bytes 2246784 | tf_op jit(solution)/shard_map/bgqt,btgd->bgqd/dot_general | solution.py:68
  30.0 69.8 %all-gather.2 = f32[16,34,128]{2,1,0:T(8,128)S(1)} all-gather(f32[1,34,128]{2,1,0:T(8,128)S(1)} %maximum_bitcast_fusion), channel_id=2, replica_groups=mesh['grp'=2,'seq_0'=16,'seq_1'=8,'head'=2] {'seq_0'}, dimensions={0}, use_global_device_ids=true | all-gather | bytes 295936 | tf_op jit(solution)/shard_map/all_gather | solution.py:23
  100.0 0.2 fusion.14
  100.2 26.6 %all-gather.3 = f32[8,34,128]{2,1,0:T(8,128)S(1)} all-gather(f32[1,34,128]{2,1,0:T(8,128)S(1)} %maximum_bitcast_fusion.1), channel_id=3, replica_groups=mesh['grp'=2,'seq_0'=16,'seq_1'=8,'head'=2] {'seq_1'}, dimensions={0}, use_global_device_ids=true | all-gather | bytes 156672 | tf_op jit(solution)/shard_map/all_gather | solution.py:23
  127.3 0.1 squeeze.268
  127.4 0.1 squeeze.266
  127.5 0.1 squeeze.265
  127.6 0.1 squeeze.278
  127.7 0.1 squeeze.287
  127.9 0.1 squeeze.284
  128.2 0.1 squeeze.281
  130.0 0.7 fusion.58
  (73 shorter events, 2.9 us)
Async XLA Ops:
  4.3 3.9 %copy-start.1 = (s32[2]{0:T(128)S(1)}, s32[2]{0:T(128)}, u32[]{:S(2)}) copy-start(s32[2]{0:T(128)} %param.8) | copy-start | bytes 28
  4.3 4.8 %copy-start = (bf16[2,2048]{1,0:T(2,128)(2,1)S(1)}, bf16[2,2048]{1,0:T(2,128)(2,1)}, u32[]{:S(2)}) copy-start(bf16[2,2048]{1,0:T(2,128)(2,1)} %param.7) | copy-start | bytes 24580
  4.3 8.1 %all-to-all-start = ((bf16[2,4,128,1024]{2,1,0,3:T(4,128)(2,1)}), bf16[2,4,128,1024]{2,1,0,3:T(4,128)(2,1)S(1)}, u32[]{:S(2)}, u32[]{:S(2)}) async-start(bf16[2,4,128,1024]{2,1,0,3:T(4,128)(2,1)} %copy.10), calls=%async_computation | async-start | bytes 4194304 | tf_op jit(solution)/shard_map/all_to_all | solution.py:83
  12.4 11.6 %all-to-all-start.1 = ((bf16[2,2,4,128,512]{4,3,2,1,0:T(8,128)(2,1)}), bf16[2,2,4,128,512]{4,3,2,1,0:T(8,128)(2,1)}, u32[]{:S(2)}, u32[]{:S(2)}) async-start(bf16[2,2,4,128,512]{4,3,2,1,0:T(8,128)(2,1)} %pad_maximum_fusion), calls=%async_computation.1 | async-start | bytes 4194304 | tf_op jit(solution)/shard_map/all_to_all | solution.py:85
